TPU v7x, 32 devices: a whole 2x2x4 slice. The times are simulated.
32 devices in a mesh: groups: 2 (over y), ctx: 4 (over z), ep: 2 (over x), tp: 2 (over core).
Axes of the slice: x: 2, y: 2, z: 4, core: 2. Of those that a mesh axis runs over, the one named last changes fastest.
Arguments:
- queries: bfloat16 [4, 512, 5120], P(('groups', 'ep'), 'ctx', 'tp'), parts along dimension 0, may hold values from -128 to 128
- keys: bfloat16 [4, 512, 1024], P(('groups', 'ep'), 'ctx', 'tp'), parts along dimension 0, may hold values from -6 to 6
- values: bfloat16 [4, 512, 1024], P(('groups', 'ep'), 'ctx', 'tp'), parts along dimension 0, may hold values from -6 to 6
- expert_ids: int32 [4, 512, 1], P(('groups', 'ep'), 'ctx'), parts along dimension 0, may hold values from 0 to 127, as said below
- router: bfloat16 [5120, 2], P('tp', 'ep'), may hold values from -0.3125 to 0.3125
- w_gate: bfloat16 [2, 5120, 4096], P('ep', 'tp', 'ctx'), may hold values from -0.3125 to 0.3125
- w_up: bfloat16 [2, 5120, 4096], P('ep', 'tp', 'ctx'), may hold values from -0.3125 to 0.3125
- w_down: bfloat16 [2, 4096, 5120], P('ep', 'ctx', 'tp'), may hold values from -0.09375 to 0.09375
Outputs:
- layer_out: bfloat16 [4, 512, 5120], P(('groups', 'ep'), 'ctx', 'tp'), parts along dimension 0
There are 2 independent parts, one for each index of `groups`. A program takes and returns all parts, laid end to end along the dimension named above; an argument that names none is the same for every part. Nothing has to cross between parts.
Inputs may be any that keep to these rules, and one draw needn't show every extreme that they name: `expert_ids`: among the positions of one device, each expert below 2 is named at most 2 times; in every draw one of them is named exactly 2 times on every device.
All inputs are finite; a program needn't handle non-finite values.
Results may differ from a plain program's by a relative error of at most 0.023.
Values may be sent and summed in bfloat16 or wider, within the bound.
A program may use at most 64 MiB of HBM per device.

v0:
```python
import jax
import jax.numpy as jnp
from jax import lax
from jax.sharding import PartitionSpec as P

HEAD_WIDTH = 128
CAP = 2


def block_width(key_count):
    for candidate in (512, 256, 128):
        return candidate
    return key_count


def fresh_state(query_rows, kv_heads, group_width):
    return (
        jnp.full((kv_heads, group_width, query_rows), -1e30, jnp.float32),
        jnp.zeros((kv_heads, group_width, query_rows), jnp.float32),
        jnp.zeros((query_rows, kv_heads, group_width, HEAD_WIDTH), jnp.float32),
    )


def absorb_block(status, query_half, query_pos, key_block, value_block, key_pos):
    old_max, totals, weighted = status
    scores = jnp.einsum(
        "rgqd,kgd->gqrk", query_half, key_block, preferred_element_type=jnp.float32
    ) * HEAD_WIDTH ** (-0.5)
    visible = query_pos[:, None] >= key_pos[None, :]
    scores = jnp.where(visible, scores, -1e30)
    running_max = jnp.maximum(old_max, jnp.max(scores, axis=3))
    factor = jnp.exp(old_max - running_max)
    weights = jnp.where(visible, jnp.exp(scores - running_max[..., None]), 0.0)
    totals = totals * factor + jnp.sum(weights, axis=3)
    update = jnp.einsum(
        "gqrk,kgd->rgqd",
        weights.astype(jnp.bfloat16),
        value_block,
        preferred_element_type=jnp.float32,
    )
    weighted = weighted * jnp.transpose(factor, (2, 0, 1))[..., None] + update
    return (running_max, totals, weighted)


def finish(status, row_count):
    old_max, totals, weighted = status
    normed = weighted / jnp.transpose(totals, (2, 0, 1))[..., None]
    return normed.astype(jnp.bfloat16).reshape(row_count, -1)


def shards(queries, keys, values, expert_ids, router, w_gate, w_up, w_down):
    row_count = queries.shape[1]
    half_rows = row_count // 2
    feature_width = queries.shape[2]
    kv_heads = keys.shape[2] // HEAD_WIDTH
    group_width = feature_width // HEAD_WIDTH // kv_heads
    ep_count = lax.axis_size("ep")
    ctx_place = lax.axis_index("ctx")
    local_queries = queries[0].reshape(row_count, kv_heads, group_width, HEAD_WIDTH)
    lead_half = local_queries[:half_rows]
    tail_half = local_queries[half_rows:]
    lead_pos = ctx_place * row_count + jnp.arange(half_rows, dtype=jnp.int32)
    tail_pos = ctx_place * row_count + half_rows + jnp.arange(half_rows, dtype=jnp.int32)
    initial = (
        fresh_state(half_rows, kv_heads, group_width),
        fresh_state(half_rows, kv_heads, group_width),
    )
    key_piece = lax.all_gather(keys, "ctx", axis=1, tiled=True)[0]
    key_count = key_piece.shape[0]
    key_block_rows = block_width(key_count)
    block_count = key_count // key_block_rows
    key_blocks = key_piece.reshape(block_count, key_block_rows, kv_heads, HEAD_WIDTH)
    value_blocks = lax.all_gather(values, "ctx", axis=1, tiled=True)[0].reshape(
        block_count, key_block_rows, kv_heads, HEAD_WIDTH
    )
    offsets = jnp.arange(block_count, dtype=jnp.int32) * key_block_rows

    def one_block(status, inputs):
        key_block, value_block, block_begin = inputs
        key_pos = block_begin + jnp.arange(key_block_rows, dtype=jnp.int32)
        lead_state = lax.cond(
            block_begin <= lead_pos[-1],
            lambda kept_state: absorb_block(
                kept_state, lead_half, lead_pos, key_block, value_block, key_pos
            ),
            lambda kept_state: kept_state,
            status[0],
        )
        tail_state = lax.cond(
            block_begin <= tail_pos[-1],
            lambda kept_state: absorb_block(
                kept_state, tail_half, tail_pos, key_block, value_block, key_pos
            ),
            lambda kept_state: kept_state,
            status[1],
        )
        return ((lead_state, tail_state), None)

    result, _ = lax.scan(one_block, initial, (key_blocks, value_blocks, offsets))
    lead_status, tail_status = result
    lead_out = finish(lead_status, half_rows)
    tail_out = finish(tail_status, half_rows)
    attended = jnp.concatenate([lead_out, tail_out], axis=0)
    chosen = expert_ids[0, :, 0]
    choose = (chosen[:, None] == jnp.arange(ep_count, dtype=jnp.int32)[None, :]).astype(jnp.int32)
    earlier = jnp.cumsum(choose, axis=0) - choose
    slot_index = jnp.sum(earlier * choose, axis=1)
    target = chosen * CAP + slot_index
    spread = (target[None, :] == jnp.arange(ep_count * CAP, dtype=jnp.int32)[:, None]).astype(
        jnp.bfloat16
    )
    outgoing = jnp.dot(spread, attended, preferred_element_type=jnp.float32).astype(jnp.bfloat16)
    arrived = lax.all_to_all(
        outgoing.reshape(ep_count, CAP, feature_width),
        "ep",
        split_axis=0,
        concat_axis=0,
        tiled=True,
    )
    gathered = lax.all_gather(arrived[None], "ctx", axis=0, tiled=True)
    members = gathered.reshape(-1, feature_width)
    gate_w = w_gate[0]
    up_w = w_up[0]
    down_w = w_down[0]
    gate_part = jnp.dot(members, gate_w, preferred_element_type=jnp.float32)
    up_part = jnp.dot(members, up_w, preferred_element_type=jnp.float32)
    score_part = jnp.dot(members, router, preferred_element_type=jnp.float32)
    gate_sum, up_sum, router_score = (
        lax.psum(gate_part.astype(jnp.bfloat16), "tp").astype(jnp.float32),
        lax.psum(up_part.astype(jnp.bfloat16), "tp").astype(jnp.float32),
        lax.psum(score_part.astype(jnp.bfloat16), "tp").astype(jnp.float32),
    )
    weight = jax.nn.sigmoid(router_score)
    hidden = (jax.nn.silu(weight * gate_sum) * (weight * up_sum)).astype(jnp.bfloat16)
    expert_rows = lax.psum_scatter(
        jnp.dot(hidden, down_w, preferred_element_type=jnp.float32).astype(jnp.bfloat16),
        "ctx",
        scatter_dimension=0,
        tiled=True,
    )
    returned = lax.all_to_all(
        expert_rows.reshape(ep_count, CAP, feature_width),
        "ep",
        split_axis=0,
        concat_axis=0,
        tiled=True,
    )
    returned = returned.reshape(ep_count * CAP, feature_width)
    routed = lax.dot_general(
        spread, returned, (((0,), (0,)), ((), ())), preferred_element_type=jnp.float32
    )
    layer_out = (attended.astype(jnp.float32) + routed).astype(jnp.bfloat16)
    return layer_out[None]


def solution(mesh):
    placed = (
        P(("groups", "ep"), "ctx", "tp"),
        P(("groups", "ep"), "ctx", "tp"),
        P(("groups", "ep"), "ctx", "tp"),
        P(("groups", "ep"), "ctx", None),
        P("tp", "ep"),
        P("ep", "tp", "ctx"),
        P("ep", "tp", "ctx"),
        P("ep", "ctx", "tp"),
    )
    return jax.shard_map(
        shards,
        mesh=mesh,
        in_specs=placed,
        out_specs=P(("groups", "ep"), "ctx", "tp"),
        check_vma=False,
    )
```

profile of v0, /device:TPU:0, one launch (start us, length us, event | category | flops | bytes accessed | tf_op | source)
XLA Modules:
  0.0 157.5 jit_solution(6667889364840034550)
XLA Ops:
  6.5 1.0 copy.23
  7.6 16.7 %all_gather.9 = bf16[1,512,512]{1,2,0:T(8,128)(2,1)S(1)} all-gather(bf16[1,128,512]{1,2,0:T(8,128)(2,1)S(1)} %copy.23), channel_id=1, replica_groups=mesh['groups'=2,'ctx'=4,'ep'=2,'tp'=2] {'ctx'}, dimensions={1}, use_global_device_ids=true | all-gather | bytes 655360 | tf_op jit(solution)/shard_map/all_gather | solution.py:68
  24.3 1.0 copy.24
  25.3 14.6 %all_gather.10 = bf16[1,512,512]{1,2,0:T(8,128)(2,1)S(1)} all-gather(bf16[1,128,512]{1,2,0:T(8,128)(2,1)S(1)} %copy.24), channel_id=1, replica_groups=mesh['groups'=2,'ctx'=4,'ep'=2,'tp'=2] {'ctx'}, dimensions={1}, use_global_device_ids=true | all-gather | bytes 655360 | tf_op jit(solution)/shard_map/all_gather | solution.py:73
  39.9 0.6 slice.23
  41.1 0.1 broadcast.44
  41.2 0.6 broadcast.43
  41.8 4.8 %conditional.3 = (f32[4,5,64]{2,1,0:T(8,128)S(1)}, f32[64,4,5,128]{3,0,2,1:T(8,128)S(1)}) conditional(s32[]{:T(128)} %bitcast.14, (f32[4,5,64]{2,1,0:T(8,128)}, f32[64,4,5,128]{3,0,2,1:T(8,128)S(1)}) %tuple.31, (s32[64]{0:T(128)S(1)}, s32[512]{0:T(512)S(1)}, bf16[1,128,2560]{2,1,0:T(8,128)(2,1)}, bf16[512,4,128]{0,2,1:T(8,128)(2,1)S(1)}, ...), branch_computations={%region_4.5_spmd, %region_5.0_spmd} | conditional | flops 344428288 | bytes 12067088 | solution.py:89
  41.8 0.1 broadcast_compare_fusion.1
  41.9 1.0 slice.18
  42.9 0.4 slice.19
  43.3 0.7 fusion.20
  44.0 0.9 fusion.22
  44.9 0.7 multiply_add_fusion.1
  45.6 1.1 fusion.29
  46.7 0.2 divide_convert_fusion
  46.9 0.2 copy.30
  47.2 0.4 reshape.57
  47.6 0.6 slice.22
  48.8 5.9 %conditional.2 = ((f32[4,5,64]{2,1,0:T(8,128)}, f32[64,4,5,128]{3,0,2,1:T(8,128)S(1)})) conditional(s32[]{:T(128)} %bitcast.10, (f32[4,5,64]{2,1,0:T(8,128)}, f32[64,4,5,128]{3,0,2,1:T(8,128)S(1)}) %tuple.31, (s32[64]{0:T(128)S(1)}, s32[512]{0:T(512)S(1)}, bf16[1,128,2560]{2,1,0:T(8,128)(2,1)S(1)}, bf16[512,4,128]{0,2,1:T(8,128)(2,1)S(1)}, ...), branch_computations={%region_0.1_spmd, %region_1.4_spmd} | conditional | flops 344428288 | bytes 12239212 | solution.py:81
  48.8 0.7 broadcast_compare_fusion
  49.6 0.4 slice.17
  50.0 1.4 fusion
  51.4 0.9 fusion.2
  52.3 1.3 multiply_add_fusion
  53.6 1.1 fusion.9
  54.7 1.0 divide_convert_fusion.1
  55.7 0.2 copy.27
  55.9 0.4 reshape.56
  56.4 0.1 fusion.59
  56.4 0.2 reduce_window_sum.11
  56.6 0.2 select_reduce_fusion
  56.8 0.2 convolution_convert_fusion
  57.1 6.4 %all_to_all.10 = bf16[2,2,2560]{2,1,0:T(2,128)(2,1)S(1)} all-to-all(bf16[2,2,2560]{2,1,0:T(2,128)(2,1)S(1)} %reshape.58), channel_id=1, replica_groups=mesh['groups'=2,'ctx'=4,'ep'=2,'tp'=2] {'ep'}, dimensions={0} | all-to-all | bytes 40960 | tf_op jit(solution)/shard_map/all_to_all | solution.py:113
  63.5 13.2 %all-gather = bf16[8,2,2560]{2,1,0:T(2,128)(2,1)S(1)} all-gather(bf16[2,2,2560]{2,1,0:T(2,128)(2,1)S(1)} %all_to_all.10), channel_id=2, replica_groups=mesh['groups'=2,'ctx'=4,'ep'=2,'tp'=2] {'ctx'}, dimensions={0}, use_global_device_ids=true | all-gather | bytes 102400 | tf_op jit(solution)/shard_map/all_gather | solution.py:120
  76.7 3.9 %fusion.51 = bf16[16,1024]{1,0:T(8,128)(2,1)} fusion(bf16[16,2560]{1,0:T(8,128)(2,1)S(1)} %reshape.59, bf16[1,2560,1024]{2,1,0:T(8,128)(2,1)} %param.17), kind=kOutput, calls=%fused_computation.51 | convolution fusion | flops 83902464 | bytes 5357568 | tf_op jit(solution)/shard_map/dot_general | solution.py:125
  80.6 3.9 %fusion.54 = bf16[16,1024]{1,0:T(8,128)(2,1)} fusion(bf16[16,2560]{1,0:T(8,128)(2,1)S(1)} %reshape.59, bf16[1,2560,1024]{2,1,0:T(8,128)(2,1)} %param.18), kind=kOutput, calls=%fused_computation.52 | convolution fusion | flops 83902464 | bytes 5357568 | tf_op jit(solution)/shard_map/dot_general | solution.py:126
  84.6 0.6 fusion.58
  85.2 0.0 all-reduce.7.cloned.1.call-update
  85.2 0.0 all-reduce.5.cloned.1.call-start
  85.3 16.5 %all-reduce.7.cloned.1.call-done = (bf16[16,1024]{1,0:T(8,128)(2,1)}, bf16[16,1024]{1,0:T(8,128)(2,1)}, bf16[16,1]{0,1:T(2,128)(2,1)}) async-done(((bf16[16,1024]{1,0:T(8,128)(2,1)}, bf16[16,1024]{1,0:T(8,128)(2,1)}, bf16[16,1]{0,1:T(2,128)(2,1)}), (bf16[16,1024]{1,0:T(8,128)(2,1)}, bf16[16,1024]{1,0:T(8,128)(2,1)}, bf16[16,1]{0,1:T(2,128)(2,1)})) %all-reduce.7.cloned.1.call-update) | async-done | bytes 65584 | tf_op jit(solution)/shard_map/psum | solution.py:130
  101.8 0.7 divide_bitcast_fusion
  102.5 4.0 %fusion.48 = bf16[16,2560]{1,0:T(8,128)(2,1)} fusion(bf16[1,1024,2560]{2,1,0:T(8,128)(2,1)} %param.19, bf16[16,1024]{1,0:T(8,128)(2,1)} %get-tuple-element.178, bf16[16,1024]{1,0:T(8,128)(2,1)} %get-tuple-element.179, f32[16]{0:T(128)S(1)} %divide_bitcast_fusion), kind=kOutput, calls=%fused_computation.49 | convolution fusion | flops 84090880 | bytes 5390400 | tf_op jit(solution)/shard_map/dot_general | solution.py:136
  106.6 0.6 dynamic-slice
  107.7 34.5 %all-reduce.5.cloned.1.call-done = bf16[16,2560]{1,0:T(8,128)(2,1)} async-done(((bf16[16,2560]{1,0:T(8,128)(2,1)}), bf16[16,2560]{1,0:T(8,128)(2,1)}) %all-reduce.5.cloned.1.call-update) | async-done | bytes 81936
  142.2 0.8 constant_dynamic-slice_fusion
  143.0 6.4 %all_to_all.11 = bf16[2,2,2560]{2,1,0:T(2,128)(2,1)S(1)} all-to-all(bf16[2,2,2560]{2,1,0:T(2,128)(2,1)S(1)} %reshape.61), channel_id=1, replica_groups=mesh['groups'=2,'ctx'=4,'ep'=2,'tp'=2] {'ep'}, dimensions={0} | all-to-all | bytes 40960 | tf_op jit(solution)/shard_map/all_to_all | solution.py:141
  149.5 1.2 fusion.47
  (31 shorter events, 0.3 us)
Async XLA Ops:
  6.5 78.0 %copy-start = (bf16[2560,1]{0,1:T(2,128)(2,1)S(1)}, bf16[2560,1]{0,1:T(2,128)(2,1)}, u32[]{:S(2)}) copy-start(bf16[2560,1]{0,1:T(2,128)(2,1)} %param.16) | copy-start | bytes 15364
  6.5 95.3 %all-reduce.7.cloned.1.call-start = ((), (), s32[]{:S(2)}) async-start(), calls=%async_computation.3 | async-start | bytes 132096 | tf_op jit(solution)/shard_map/psum | solution.py:130
  46.7 2.1 %copy-start.1 = (bf16[1,128,2560]{2,1,0:T(8,128)(2,1)S(1)}, bf16[1,128,2560]{2,1,0:T(8,128)(2,1)}, u32[]{:S(2)}) copy-start(bf16[1,128,2560]{2,1,0:T(8,128)(2,1)} %param.12) | copy-start | bytes 1966084
  48.8 0.7 copy-start.2
  49.6 1.8 %copy-start.3 = (f32[4,5,64]{2,1,0:T(8,128)S(1)}, f32[4,5,64]{2,1,0:T(8,128)}, u32[]{:S(2)}) copy-start(f32[4,5,64]{2,1,0:T(8,128)} %copy-done.2) | copy-start | bytes 15364 | tf_op jit(solution)/shard_map/while/body/eval_jaxpr/cond
  49.6 1.9 %copy-start.4 = (pred[64,512]{1,0:T(8,128)(4,1)S(1)}, pred[64,512]{1,0:T(8,128)(4,1)}, u32[]{:S(2)}) copy-start(pred[64,512]{1,0:T(8,128)(4,1)} %broadcast_compare_fusion) | copy-start | bytes 98308 | tf_op jit(solution)/shard_map/while/body/eval_jaxpr/cond
  54.7 1.6 %copy-start.5 = (s32[1,128,1]{1,2,0:T(1,128)S(1)}, s32[1,128,1]{1,2,0:T(1,128)}, u32[]{:S(2)}) copy-start(s32[1,128,1]{1,2,0:T(1,128)} %param.15) | copy-start | bytes 1540
  85.2 57.0 %all-reduce.5.cloned.1.call-start = ((), (), s32[]{:S(2)}) async-start(), calls=%async_computation.2 | async-start | bytes 163840
  102.5 4.1 %copy-start.6 = (u32[32]{0:T(128)S(1)}, u32[32]{0:T(128)}, u32[]{:S(2)}) copy-start(u32[32]{0:T(128)} %constant.73) | copy-start | bytes 388
Sparse Core Ops, SparseCore 0:
  85.3 16.4 all-reduce.6
  106.7 35.4 all-reduce.4
where the time goes:
time: 158 us
  blocking collectives  57.4 us (36%)
  waiting for transfers between devices  51.1 us (32%)
  matrix products  18.1 us (11%)
  between operations  15.5 us (10%)
  local copies, waits for them, and re-layouts  8.44 us (5%)
  other arithmetic  6.94 us (4%)
    unnamed x3, waiting for transfers between devices  34.5 us
    all_gather x1, blocking collectives, shards(): key_piece = lax.all_gather(keys, 'ctx', axis=1, tiled=True)[0]  16.7 us
    psum x1, waiting for transfers between devices, shards(): lax.psum(up_part.astype(jnp.bfloat16), 'tp').astype(jnp.float32)  16.5 us
    all_gather x1, blocking collectives, shards(): lax.all_gather(values, 'ctx', axis=1, tiled=True)[0]  14.6 us
    all_gather x1, blocking collectives, shards(): gathered = lax.all_gather(arrived[None], 'ctx', axis=0, tiled=True)  13.2 us
    all_to_all x1, blocking collectives, shards(): lax.all_to_all(outgoing.reshape(ep_count, CAP, feature_width), 'ep', spli...  6.44 us
    all_to_all x1, blocking collectives, shards(): lax.all_to_all(expert_rows.reshape(ep_count, CAP, feature_width), 'ep', s...  6.41 us
    dot_general x1, matrix products, shards(): jnp.dot(hidden, down_w, preferred_element_type=jnp.float32)  4.03 us
  transfers between devices with their start and end apart: 2, of which 2 were waited for; matrix products, arithmetic and copies ran while one was open for 0% of the time, Pallas kernels for 0%

commit v1 on v0

--- a/solution.py
+++ b/solution.py
@@ -127,7 +127,7 @@
     score_part = jnp.dot(members, router, preferred_element_type=jnp.float32)
     gate_sum, up_sum, router_score = (
         lax.psum(gate_part.astype(jnp.bfloat16), "tp").astype(jnp.float32),
-        lax.psum(up_part.astype(jnp.bfloat16), "tp").astype(jnp.float32),
+        jnp.sum(lax.all_gather(up_part.astype(jnp.bfloat16), "tp"), axis=0).astype(jnp.float32),
         lax.psum(score_part.astype(jnp.bfloat16), "tp").astype(jnp.float32),
     )
     weight = jax.nn.sigmoid(router_score)

time: 158 us -> 142 us (0.90)
  waiting for transfers between devices: 51.1 us -> 31.7 us
  blocking collectives: 57.4 us -> 62.7 us
  matrix products: 18.1 us -> 16.3 us
    psum x1 -> x0, waiting for transfers between devices: 16.5 us -> none  [shards(): lax.psum(up_part.astype(jnp.bfloat16), 'tp').astype(jnp.float32)]
    psum x0 -> x1, blocking collectives: none -> 3.46 us  [shards(): lax.psum(gate_part.astype(jnp.bfloat16), 'tp').astype(jnp.float32)]
    unnamed x3 -> x2, waiting for transfers between devices: 34.5 us -> 31.7 us
    all_gather x0 -> x1, blocking collectives: none -> 1.85 us  [shards(): lax.all_gather(up_part.astype(jnp.bfloat16), 'tp')]
  transfers between devices with their start and end apart: 2 -> 1, of which waited for: 2 -> 1; matrix products, arithmetic and copies ran while one was open for 0% -> 0% of each run, Pallas kernels for 0% -> 0%
where the time goes in v1:
time: 142 us; the launch traced here: 141 us
  blocking collectives  62.7 us (44%)
  waiting for transfers between devices  31.7 us (22%)
  matrix products  16.3 us (11%)
  between operations  15.5 us (11%)
  local copies, waits for them, and re-layouts  8.46 us (6%)
  other arithmetic  6.27 us (4%)
    unnamed x2, waiting for transfers between devices  31.7 us
    all_gather x1, blocking collectives, shards(): key_piece = lax.all_gather(keys, 'ctx', axis=1, tiled=True)[0]  16.7 us
    all_gather x1, blocking collectives, shards(): lax.all_gather(values, 'ctx', axis=1, tiled=True)[0]  14.6 us
    all_gather x1, blocking collectives, shards(): gathered = lax.all_gather(arrived[None], 'ctx', axis=0, tiled=True)  13.2 us
    all_to_all x1, blocking collectives, shards(): lax.all_to_all(outgoing.reshape(ep_count, CAP, feature_width), 'ep', spli...  6.44 us
    all_to_all x1, blocking collectives, shards(): lax.all_to_all(expert_rows.reshape(ep_count, CAP, feature_width), 'ep', s...  6.42 us
    dot_general x1, matrix products, shards(): jnp.dot(hidden, down_w, preferred_element_type=jnp.float32)  3.98 us
    unnamed x13, local copies, waits for them, and re-layouts  3.47 us
  transfers between devices with their start and end apart: 1, of which 1 were waited for; matrix products, arithmetic and copies ran while one was open for 0% of the time, Pallas kernels for 0%

profile of v1, /device:TPU:0, one launch (start us, length us, event | category | flops | bytes accessed | tf_op | source)
XLA Modules:
  0.0 141.0 jit_solution(17248721225384586135)
XLA Ops:
  6.5 1.0 copy.23
  7.6 16.7 %all_gather.15 = bf16[1,512,512]{1,2,0:T(8,128)(2,1)S(1)} all-gather(bf16[1,128,512]{1,2,0:T(8,128)(2,1)S(1)} %copy.23), channel_id=1, replica_groups=mesh['groups'=2,'ctx'=4,'ep'=2,'tp'=2] {'ctx'}, dimensions={1}, use_global_device_ids=true | all-gather | bytes 655360 | tf_op jit(solution)/shard_map/all_gather | solution.py:68
  24.3 1.0 copy.24
  25.3 14.6 %all_gather.16 = bf16[1,512,512]{1,2,0:T(8,128)(2,1)S(1)} all-gather(bf16[1,128,512]{1,2,0:T(8,128)(2,1)S(1)} %copy.24), channel_id=1, replica_groups=mesh['groups'=2,'ctx'=4,'ep'=2,'tp'=2] {'ctx'}, dimensions={1}, use_global_device_ids=true | all-gather | bytes 655360 | tf_op jit(solution)/shard_map/all_gather | solution.py:73
  39.9 0.6 slice.23
  41.1 0.1 broadcast.44
  41.2 0.6 broadcast.43
  41.8 4.8 %conditional.3 = (f32[4,5,64]{2,1,0:T(8,128)S(1)}, f32[64,4,5,128]{3,0,2,1:T(8,128)S(1)}) conditional(s32[]{:T(128)} %bitcast.14, (f32[4,5,64]{2,1,0:T(8,128)}, f32[64,4,5,128]{3,0,2,1:T(8,128)S(1)}) %tuple.31, (s32[64]{0:T(128)S(1)}, s32[512]{0:T(512)S(1)}, bf16[1,128,2560]{2,1,0:T(8,128)(2,1)}, bf16[512,4,128]{0,2,1:T(8,128)(2,1)S(1)}, ...), branch_computations={%region_4.5_spmd, %region_5.0_spmd} | conditional | flops 344428288 | bytes 12067088 | solution.py:89
  41.8 0.1 broadcast_compare_fusion.1
  41.9 1.0 slice.18
  42.9 0.4 slice.19
  43.3 0.7 fusion.20
  44.0 0.9 fusion.22
  44.9 0.7 multiply_add_fusion.1
  45.6 1.1 fusion.29
  46.7 0.2 divide_convert_fusion
  46.9 0.2 copy.30
  47.2 0.4 reshape.57
  47.5 0.6 slice.22
  48.8 5.9 %conditional.2 = ((f32[4,5,64]{2,1,0:T(8,128)}, f32[64,4,5,128]{3,0,2,1:T(8,128)S(1)})) conditional(s32[]{:T(128)} %bitcast.10, (f32[4,5,64]{2,1,0:T(8,128)}, f32[64,4,5,128]{3,0,2,1:T(8,128)S(1)}) %tuple.31, (s32[64]{0:T(128)S(1)}, s32[512]{0:T(512)S(1)}, bf16[1,128,2560]{2,1,0:T(8,128)(2,1)S(1)}, bf16[512,4,128]{0,2,1:T(8,128)(2,1)S(1)}, ...), branch_computations={%region_0.1_spmd, %region_1.4_spmd} | conditional | flops 344428288 | bytes 12239212 | solution.py:81
  48.8 0.7 broadcast_compare_fusion
  49.6 0.4 slice.17
  50.0 1.4 %fusion = (f32[4,5,64]{2,1,0:T(8,128)S(1)}, f32[4,512,64,5]{1,2,3,0:T(8,128)S(1)}) fusion(pred[64,512]{1,0:T(8,128)(4,1)} %broadcast_compare_fusion, bf16[64,4,5,128]{3,2,1,0:T(8,128)(2,1)S(1)} %slice.17, bf16[512,4,128]{0,2,1:T(8,128)(2,1)S(1)} %get-tuple-element.165), kind=kOutput, calls=%fused_computation.2 | convolution fusion | flops 169736960 | bytes 3511296 | tf_op jit(solution)/shard_map/while/body/eval_jaxpr/cond/branch_1_fun/rgqd,kgd->gqrk/dot_general | solution.py:26
  51.4 0.9 fusion.2
  52.3 1.3 multiply_add_fusion
  53.6 1.1 fusion.9
  54.7 1.0 divide_convert_fusion.1
  55.7 0.2 copy.27
  55.9 0.4 reshape.56
  56.3 0.1 fusion.59
  56.4 0.2 reduce_window_sum.11
  56.6 0.2 select_reduce_fusion
  56.8 0.2 convolution_convert_fusion
  57.0 6.4 %all_to_all.10 = bf16[2,2,2560]{2,1,0:T(2,128)(2,1)S(1)} all-to-all(bf16[2,2,2560]{2,1,0:T(2,128)(2,1)S(1)} %reshape.58), channel_id=1, replica_groups=mesh['groups'=2,'ctx'=4,'ep'=2,'tp'=2] {'ep'}, dimensions={0} | all-to-all | bytes 40960 | tf_op jit(solution)/shard_map/all_to_all | solution.py:113
  63.5 13.2 %all-gather = bf16[8,2,2560]{2,1,0:T(2,128)(2,1)S(1)} all-gather(bf16[2,2,2560]{2,1,0:T(2,128)(2,1)S(1)} %all_to_all.10), channel_id=2, replica_groups=mesh['groups'=2,'ctx'=4,'ep'=2,'tp'=2] {'ctx'}, dimensions={0}, use_global_device_ids=true | all-gather | bytes 102400 | tf_op jit(solution)/shard_map/all_gather | solution.py:120
  76.7 3.3 %fusion.51 = bf16[16,1024]{1,0:T(8,128)(2,1)S(1)} fusion(bf16[16,2560]{1,0:T(8,128)(2,1)S(1)} %reshape.59, bf16[1,2560,1024]{2,1,0:T(8,128)(2,1)} %param.17), kind=kOutput, calls=%fused_computation.51 | convolution fusion | flops 83902464 | bytes 5357568 | tf_op jit(solution)/shard_map/dot_general | solution.py:125
  80.0 0.1 fusion.58
  80.2 3.5 %all-reduce.1 = (bf16[16,1024]{1,0:T(8,128)(2,1)S(1)}, bf16[16,1]{0,1:T(2,128)(2,1)S(1)}) all-reduce(bf16[16,1024]{1,0:T(8,128)(2,1)S(1)} %fusion.51, bf16[16,1]{0,1:T(2,128)(2,1)S(1)} %fusion.58), channel_id=1, replica_groups=mesh['groups'=2,'ctx'=4,'ep'=2,'tp'=2] {'tp'}, use_global_device_ids=true, to_apply=%region_11.12 | all-reduce | flops 16400 | bytes 65600 | tf_op jit(solution)/shard_map/psum | solution.py:129
  83.6 3.3 %fusion.54 = bf16[16,1024]{1,0:T(8,128)(2,1)S(1)} fusion(bf16[16,2560]{1,0:T(8,128)(2,1)S(1)} %reshape.59, bf16[1,2560,1024]{2,1,0:T(8,128)(2,1)} %param.18), kind=kOutput, calls=%fused_computation.52 | convolution fusion | flops 83902464 | bytes 5357568 | tf_op jit(solution)/shard_map/dot_general | solution.py:126
  86.9 1.8 %all-gather.1 = bf16[32,1024]{1,0:T(8,128)(2,1)S(1)} all-gather(bf16[16,1024]{1,0:T(8,128)(2,1)S(1)} %fusion.54), channel_id=3, replica_groups=mesh['groups'=2,'ctx'=4,'ep'=2,'tp'=2] {'tp'}, dimensions={0}, use_global_device_ids=true | all-gather | bytes 98304 | tf_op jit(solution)/shard_map/all_gather | solution.py:130
  88.8 0.0 copy-start.6
  88.8 4.0 %fusion.48 = bf16[16,2560]{1,0:T(8,128)(2,1)} fusion(bf16[1,1024,2560]{2,1,0:T(8,128)(2,1)} %param.19, bf16[16,1024]{1,0:T(8,128)(2,1)S(1)} %reduce_sum.42, bf16[16,1024]{1,0:T(8,128)(2,1)S(1)} %get-tuple-element.178, f32[16]{0:T(128)S(1)} %divide_bitcast_fusion), kind=kOutput, calls=%fused_computation.49 | convolution fusion | flops 84090880 | bytes 5390400 | tf_op jit(solution)/shard_map/dot_general | solution.py:136
  92.8 0.0 all-reduce.4.cloned.1.call-update
  92.8 0.6 dynamic-slice
  94.0 31.6 %all-reduce.4.cloned.1.call-done = bf16[16,2560]{1,0:T(8,128)(2,1)} async-done(((bf16[16,2560]{1,0:T(8,128)(2,1)}), bf16[16,2560]{1,0:T(8,128)(2,1)}) %all-reduce.4.cloned.1.call-update) | async-done | bytes 81936
  125.7 0.8 constant_dynamic-slice_fusion
  126.5 6.4 %all_to_all.11 = bf16[2,2,2560]{2,1,0:T(2,128)(2,1)S(1)} all-to-all(bf16[2,2,2560]{2,1,0:T(2,128)(2,1)S(1)} %reshape.61), channel_id=1, replica_groups=mesh['groups'=2,'ctx'=4,'ep'=2,'tp'=2] {'ep'}, dimensions={0} | all-to-all | bytes 40960 | tf_op jit(solution)/shard_map/all_to_all | solution.py:141
  132.9 1.2 fusion.47
  (31 shorter events, 0.3 us)
Async XLA Ops:
  6.5 73.5 %copy-start = (bf16[2560,1]{0,1:T(2,128)(2,1)S(1)}, bf16[2560,1]{0,1:T(2,128)(2,1)}, u32[]{:S(2)}) copy-start(bf16[2560,1]{0,1:T(2,128)(2,1)} %param.16) | copy-start | bytes 15364
  6.5 119.2 %all-reduce.4.cloned.1.call-start = ((), (), s32[]{:S(2)}) async-start(), calls=%async_computation.2 | async-start | bytes 163840
  46.7 2.1 %copy-start.1 = (bf16[1,128,2560]{2,1,0:T(8,128)(2,1)S(1)}, bf16[1,128,2560]{2,1,0:T(8,128)(2,1)}, u32[]{:S(2)}) copy-start(bf16[1,128,2560]{2,1,0:T(8,128)(2,1)} %param.12) | copy-start | bytes 1966084
  48.8 0.7 copy-start.2
  49.6 1.8 %copy-start.3 = (f32[4,5,64]{2,1,0:T(8,128)S(1)}, f32[4,5,64]{2,1,0:T(8,128)}, u32[]{:S(2)}) copy-start(f32[4,5,64]{2,1,0:T(8,128)} %copy-done.2) | copy-start | bytes 15364 | tf_op jit(solution)/shard_map/while/body/eval_jaxpr/cond
  49.6 1.9 %copy-start.4 = (pred[64,512]{1,0:T(8,128)(4,1)S(1)}, pred[64,512]{1,0:T(8,128)(4,1)}, u32[]{:S(2)}) copy-start(pred[64,512]{1,0:T(8,128)(4,1)} %broadcast_compare_fusion) | copy-start | bytes 98308 | tf_op jit(solution)/shard_map/while/body/eval_jaxpr/cond
  54.7 1.6 %copy-start.5 = (s32[1,128,1]{1,2,0:T(1,128)S(1)}, s32[1,128,1]{1,2,0:T(1,128)}, u32[]{:S(2)}) copy-start(s32[1,128,1]{1,2,0:T(1,128)} %param.15) | copy-start | bytes 1540
  88.8 4.0 %copy-start.6 = (u32[32]{0:T(128)S(1)}, u32[32]{0:T(128)}, u32[]{:S(2)}) copy-start(u32[32]{0:T(128)} %constant.76) | copy-start | bytes 388
Sparse Core Ops, SparseCore 0:
  92.9 32.7 all-reduce.3
